TPU v7x, 32 devices: a whole 2x2x4 slice. The times are simulated.
32 devices in a mesh: beam: 2 (over x), gx: 16 (over z, y, core).
Axes of the slice: x: 2, y: 2, z: 4, core: 2. Of those that a mesh axis runs over, the one named last changes fastest.
Arguments:
- filterbank: bfloat16 [4096, 2048], P(('beam', 'gx')), parts along dimension 0, may hold values from -61 to 61
- chan_delay: int32 [16, 2048], P(None, 'gx'), may hold values from 0 to 7
- sub_delay: int32 [1536, 64], replicated, may hold values from 0 to 15
- widths: int32 [1536], replicated, may hold values from 1 to 16
Outputs:
- snr: float32 [3072, 2048], P('beam', 'gx'), parts along dimension 0
There are 2 independent parts, one for each index of `beam`. A program takes and returns all parts, laid end to end along the dimension named above; an argument that names none is the same for every part. Nothing has to cross between parts.
All inputs are finite; a program needn't handle non-finite values.
Results may differ from a plain program's by a relative error of at most 0.00059.
Values may be sent and summed in bfloat16 or wider, within the bound.
No kernel may reach another device: no remote copies, remote signals or barrier semaphores. Data moves between devices by JAX's collectives and lax.ppermute only.
A program may use at most 128 MiB of HBM per device.

v0:
```python
import jax
import jax.numpy as jnp
from jax import lax
from jax.sharding import PartitionSpec as P

SUBCH = 32
DELAY_ONE = 8
DELAY_TWO = 16
WMAX = 16


def passed_along(block, axis, distance):
    devices = range(lax.axis_size(axis))
    route = [(i - distance, i) for i in devices if i - distance in devices]
    return lax.ppermute(block, axis, route)


def per_device(filterbank, chan_delay, sub_delay, widths):
    chan_count, samples = filterbank.shape
    groups = chan_delay.shape[0]
    device_count = lax.axis_size("gx")
    sub_count = chan_count // SUBCH
    slab_len = samples // device_count
    trials, band_count = sub_delay.shape
    per_group = trials // groups
    margin_len = DELAY_TWO + WMAX
    span_len = slab_len + WMAX
    padded = jnp.pad(filterbank, ((0, 0), (0, DELAY_ONE)))
    band_input = padded.reshape(sub_count, SUBCH, samples + DELAY_ONE)
    band_delays = jnp.transpose(chan_delay.reshape(groups, sub_count, SUBCH), (1, 0, 2))
    first_codes = jnp.arange(DELAY_ONE, dtype=jnp.int32)[None, :, None]

    def band_sum(inputs):
        band_rows, delay_rows = inputs
        stacked = jnp.stack(
            [band_rows[:, offset : offset + samples] for offset in range(DELAY_ONE)], 0
        )
        stacked = stacked.reshape(DELAY_ONE * SUBCH, samples)
        one_hot = (
            (delay_rows[:, None, :] == first_codes)
            .astype(jnp.bfloat16)
            .reshape(groups, DELAY_ONE * SUBCH)
        )
        return jnp.dot(one_hot, stacked, preferred_element_type=jnp.float32).astype(jnp.bfloat16)

    subbands = lax.map(band_sum, (band_input, band_delays))
    regrouped = lax.all_to_all(subbands, "gx", split_axis=2, concat_axis=0, tiled=True)
    following = passed_along(regrouped[:, :, :margin_len], "gx", -1)
    extended = jnp.concatenate([regrouped, following], 2)
    trial_delays = sub_delay.reshape(groups, per_group, band_count)
    second_codes = jnp.arange(DELAY_TWO, dtype=jnp.int32)[None, :, None]

    def group_series(inputs):
        group_index, delay_rows = inputs
        group_rows = lax.dynamic_index_in_dim(extended, group_index, 1, keepdims=False)
        stacked = jnp.stack(
            [group_rows[:, offset : offset + span_len] for offset in range(DELAY_TWO)], 0
        )
        stacked = stacked.reshape(DELAY_TWO * band_count, span_len)
        one_hot = (
            (delay_rows[:, None, :] == second_codes)
            .astype(jnp.bfloat16)
            .reshape(per_group, DELAY_TWO * band_count)
        )
        own_part = jnp.dot(one_hot, stacked[:, :slab_len], preferred_element_type=jnp.float32)
        tail_part = lax.dot_general(
            stacked[:, slab_len:],
            one_hot,
            (((0,), (1,)), ((), ())),
            preferred_element_type=jnp.float32,
        )
        return (own_part, tail_part)

    own_blocks, tail_blocks = lax.map(
        group_series, (jnp.arange(groups, dtype=jnp.int32), trial_delays)
    )
    own_series = own_blocks.reshape(trials, slab_len)
    tail_cols = jnp.transpose(tail_blocks, (0, 2, 1)).reshape(trials, WMAX)
    series = jnp.concatenate([own_series, tail_cols], 1)
    boxcar = jnp.zeros((trials, slab_len), jnp.float32)
    for offset in range(WMAX):
        boxcar = boxcar + jnp.where(
            offset < widths[:, None], series[:, offset : offset + slab_len], 0.0
        )
    totals, squares = lax.psum(
        (jnp.sum(own_series, axis=1), jnp.sum(own_series * own_series, axis=1)), "gx"
    )
    average = totals / samples
    variance = squares / samples - average * average
    width_float = widths.astype(jnp.float32)[:, None]
    return (boxcar - width_float * average[:, None]) / jnp.sqrt(
        width_float * (variance[:, None] + 1e-05)
    )


def solution(mesh):
    in_specs = (P(("beam", "gx"), None), P(None, "gx"), P(), P())
    out_specs = P("beam", "gx")
    return jax.shard_map(
        per_device, mesh=mesh, in_specs=in_specs, out_specs=out_specs, check_vma=False
    )
```

profile of v0, /device:TPU:0, one launch (start us, length us, event | category | flops | bytes accessed | tf_op | source)
XLA Modules:
  0.0 178.5 jit_solution(11185816409424602314)
XLA Ops:
  0.0 0.8 reshape.68
  0.8 1.1 pad.4
  1.9 4.6 %while.24 = (s32[]{:T(128)}, bf16[4,16,2048]{2,1,0:T(8,128)(2,1)S(1)}, s32[4,16,32]{2,0,1:T(4,128)S(1)}, bf16[4,32,2056]{2,1,0:T(8,128)(2,1)S(1)}, s32[]{:T(128)}) while((s32[]{:T(128)}, bf16[4,16,2048]{2,1,0:T(8,128)(2,1)S(1)}, s32[4,16,32]{2,0,1:T(4,128)S(1)}, bf16[4,32,2056]{2,1,0:T(8,128)(2,1)S(1)}, s32[]{:T(128)}) %tuple.66), condition=%wide.region_1.2_spmd.clone, body=%wide.region_0.1_spmd.clone.sunk | while | flops 16814080 | bytes 3486793 | solution.py:46
  2.7 0.3 fusion.95
  3.9 0.3 fusion.95
  5.0 0.3 fusion.95
  6.2 0.3 fusion.95
  6.5 1.4 copy.16
  7.8 2.1 %reshape.74 = bf16[16,2,4096]{2,1,0:T(2,128)(2,1)S(1)} reshape(bf16[2048,4,16]{2,1,0:T(4,128)(2,1)S(1)} %bitcast.225) | data formatting | bytes 524288
  10.0 17.2 %all_to_all.18 = bf16[16,2,4096]{2,1,0:T(2,128)(2,1)S(1)} all-to-all(bf16[16,2,4096]{2,1,0:T(2,128)(2,1)S(1)} %reshape.74), channel_id=1, replica_groups=mesh['beam'=2,'gx'=16] {'gx'}, dimensions={0} | all-to-all | bytes 524288 | tf_op jit(solution)/shard_map/all_to_all | solution.py:47
  27.2 1.4 reshape.75
  28.7 1.0 copy.17
  29.7 1.3 collective-permute-start
  31.2 1.9 %collective-permute-done = bf16[64,16,32]{2,0,1:T(8,128)(2,1)S(1)} collective-permute-done((bf16[64,16,32]{2,0,1:T(8,128)(2,1)S(1)}, bf16[64,16,32]{2,0,1:T(8,128)(2,1)S(1)}, u32[]{:S(2)}, u32[]{:S(2)}) %collective-permute-start) | collective-permute-done | bytes 65568 | tf_op jit(solution)/shard_map/ppermute | solution.py:15
  33.3 70.5 %while.25 = (s32[]{:T(128)}, f32[16,96,128]{2,1,0:T(8,128)S(1)}, f32[16,16,96]{2,1,0:T(8,128)S(1)}, s32[16,96,64]{1,0,2:T(8,128)S(1)}, s32[16]{0:T(128)S(1)}, /*...) while((s32[]{:T(128)}, f32[16,96,128]{2,1,0:T(8,128)S(1)}, ...), condition=%wide.region_3.4_spmd.clone, body=%wide.region_2.3_spmd.clone.sunk | while | flops 28409860 | bytes 2107547 | solution.py:74
  33.3 0.6 dynamic_slice.38
  37.1 0.3 fusion.100
  37.4 0.2 fusion.101
  37.7 0.6 dynamic_slice.38
  41.5 0.3 fusion.100
  41.9 0.2 fusion.101
  42.1 0.6 dynamic_slice.38
  45.9 0.3 fusion.100
  46.3 0.2 fusion.101
  46.5 0.6 dynamic_slice.38
  50.3 0.3 fusion.100
  50.7 0.2 fusion.101
  50.9 0.6 dynamic_slice.38
  54.7 0.3 fusion.100
  55.1 0.2 fusion.101
  55.3 0.6 dynamic_slice.38
  59.2 0.3 fusion.100
  59.5 0.2 fusion.101
  59.7 0.6 dynamic_slice.38
  63.6 0.3 fusion.100
  63.9 0.2 fusion.101
  64.1 0.6 dynamic_slice.38
  68.0 0.3 fusion.100
  68.3 0.2 fusion.101
  68.5 0.6 dynamic_slice.38
  72.4 0.3 fusion.100
  72.7 0.2 fusion.101
  72.9 0.6 dynamic_slice.38
  76.8 0.3 fusion.100
  77.1 0.2 fusion.101
  77.3 0.6 dynamic_slice.38
  81.2 0.3 fusion.100
  81.5 0.2 fusion.101
  81.7 0.6 dynamic_slice.38
  85.6 0.3 fusion.100
  85.9 0.2 fusion.101
  86.1 0.6 dynamic_slice.38
  90.0 0.3 fusion.100
  90.3 0.2 fusion.101
  90.5 0.6 dynamic_slice.38
  94.4 0.3 fusion.100
  94.9 0.6 dynamic_slice.38
  98.8 0.3 fusion.100
  99.4 0.6 dynamic_slice.38
  103.2 0.3 fusion.100
  103.8 0.6 fusion.66
  104.5 0.3 copy.19
  104.8 61.7 %all-reduce.1 = (f32[1536]{0:T(1024)S(1)}, f32[1536]{0:T(1024)S(1)}) all-reduce(f32[1536]{0:T(1024)S(1)} %reduce_sum.25, f32[1536]{0:T(1024)S(1)} %reduce_sum.23), channel_id=1, replica_groups=mesh['beam'=2,'gx'=16] {'gx'}, use_global_device_ids=true, to_apply=%region_7.8 | all-reduce | flops 3072 | bytes 24576 | tf_op jit(solution)/shard_map/psum | solution.py:85
  166.5 11.9 %fusion.25 = f32[1536,128]{1,0:T(8,128)} fusion(f32[1536,128]{1,0:T(8,128)S(1)} %bitcast.229, f32[1536,16]{1,0:T(8,128)S(1)} %bitcast.228, f32[1536]{0:T(1024)S(1)} %get-tuple-element.146, f32[1536]{0:T(1024)S(1)} %get-tuple-element.145, pred[1536]{0:T(1024)(128)(4,1)S(1)} %get-tuple-element.162, pred[1536]{0:T(1024)(128)(4,1)S(1)} %get-tuple-element.148, ...), kind=kLoop, calls=%fused_computation.100 | loop fusion | flops 9437184 | bytes 1708032 | tf_op jit(solution)/shard_map/div | solution.py:91
  (393 shorter events, 28.9 us)
Async XLA Ops:
  27.2 3.8 %copy-start.1 = (s32[1536]{0:T(1024)S(1)}, s32[1536]{0:T(1024)}, u32[]{:S(2)}) copy-start(s32[1536]{0:T(1024)} %param.11) | copy-start | bytes 18436
  27.2 3.8 %copy-start = (s32[1536,64]{0,1:T(8,128)S(1)}, s32[1536,64]{0,1:T(8,128)}, u32[]{:S(2)}) copy-start(s32[1536,64]{0,1:T(8,128)} %param.10) | copy-start | bytes 1179652
  29.7 3.4 %collective-permute-start = (bf16[64,16,32]{2,0,1:T(8,128)(2,1)S(1)}, bf16[64,16,32]{2,0,1:T(8,128)(2,1)S(1)}, u32[]{:S(2)}, u32[]{:S(2)}) collective-permute-start(bf16[64,16,32]{2,0,1:T(8,128)(2,1)S(1)} %bitcast.231), channel_id=1, source_target_pairs={{1,0},{2,1},{3,2},{4,3},{5,4},{6,5},{7,6},{8,7},{9,8},{10,9},{11,1... | collective-permute-start | bytes 196616 | tf_op jit(solution)/shard_map/ppermute | solution.py:15
where the time goes:
time: 179 us; the launch traced here: 178 us
  blocking collectives  78.9 us (44%)
  local copies, waits for them, and re-layouts  42.3 us (24%)
  loops' own time  28.1 us (16%)
  other arithmetic  16 us (9%)
  matrix products  9.84 us (5%)
  waiting for transfers between devices  1.88 us (1%)
    psum x1, blocking collectives, per_device(): lax.psum((jnp.sum(own_series, axis=1), jnp.sum(own_series * own_series, a...  61.7 us
    another operation x1, loops' own time, per_device(): lax.map(group_series, (jnp.arange(groups, dtype=jnp.int32), trial_delays))  27.8 us
    while x268, local copies, waits for them, and re-layouts  20.8 us
    all_to_all x1, blocking collectives, per_device(): lax.all_to_all(subbands, 'gx', split_axis=2, concat_axis=0, tiled=True)  17.2 us
    div x1, other arithmetic, per_device(): (boxcar - width_float * average[:, None]) / jnp.sqrt(width_float * (varia...  11.9 us
    dynamic_slice x32, local copies, waits for them, and re-layouts, per_device(): lax.map(group_series, (jnp.arange(groups, dtype=jnp.int32), trial_delays))  9.85 us
    dot_general x16, matrix products, group_series(): jnp.dot(one_hot, stacked[:, :slab_len], preferred_element_type=jnp.float32)  5 us
  transfers between devices with their start and end apart: 1, of which 1 were waited for; matrix products, arithmetic and copies ran while one was open for 0% of the time, Pallas kernels for 0%

commit v1 on v0

--- a/solution.py
+++ b/solution.py
@@ -44,7 +44,10 @@
         return jnp.dot(one_hot, stacked, preferred_element_type=jnp.float32).astype(jnp.bfloat16)
 
     subbands = lax.map(band_sum, (band_input, band_delays))
-    regrouped = lax.all_to_all(subbands, "gx", split_axis=2, concat_axis=0, tiled=True)
+    regrouped = jnp.concatenate(
+        lax.all_to_all(jnp.stack(jnp.split(subbands, lax.axis_size("gx"), axis=2)), "gx", 0, 0),
+        axis=0,
+    )
     following = passed_along(regrouped[:, :, :margin_len], "gx", -1)
     extended = jnp.concatenate([regrouped, following], 2)
     trial_delays = sub_delay.reshape(groups, per_group, band_count)

time: 179 us -> 174 us (0.972)
  local copies, waits for them, and re-layouts: 42.3 us -> 36.6 us
    unnamed x6 -> x19, local copies, waits for them, and re-layouts: 3.58 us -> 0.19 us
    while x269 -> x268, local copies, waits for them, and re-layouts: 22.2 us -> 20.8 us
where the time goes in v1:
time: 174 us; the launch traced here: 173 us
  blocking collectives  78.9 us (45%)
  local copies, waits for them, and re-layouts  36.6 us (21%)
  loops' own time  28.1 us (16%)
  other arithmetic  16 us (9%)
  matrix products  9.84 us (6%)
  waiting for transfers between devices  1.88 us (1%)
    psum x1, blocking collectives, per_device(): lax.psum((jnp.sum(own_series, axis=1), jnp.sum(own_series * own_series, a...  61.7 us
    another operation x1, loops' own time, per_device(): lax.map(group_series, (jnp.arange(groups, dtype=jnp.int32), trial_delays))  27.8 us
    while x268, local copies, waits for them, and re-layouts  20.8 us
    all_to_all x1, blocking collectives, per_device(): lax.all_to_all(jnp.stack(jnp.split(subbands, lax.axis_size('gx'), axis=2)...  17.2 us
    div x1, other arithmetic, per_device(): (boxcar - width_float * average[:, None]) / jnp.sqrt(width_float * (varia...  11.9 us
    dynamic_slice x32, local copies, waits for them, and re-layouts, per_device(): lax.map(group_series, (jnp.arange(groups, dtype=jnp.int32), trial_delays))  9.85 us
    dot_general x16, matrix products, group_series(): jnp.dot(one_hot, stacked[:, :slab_len], preferred_element_type=jnp.float32)  5 us
    dot_general x16, matrix products, group_series(): lax.dot_general(stacked[:, slab_len:], one_hot, (((0,), (1,)), ((), ())),...  3.53 us
  transfers between devices with their start and end apart: 1, of which 1 were waited for; matrix products, arithmetic and copies ran while one was open for 0% of the time, Pallas kernels for 0%

profile of v1, /device:TPU:0, one launch (start us, length us, event | category | flops | bytes accessed | tf_op | source)
XLA Modules:
  0.0 172.9 jit_solution(4677755764921018603)
XLA Ops:
  0.0 0.8 reshape.71
  0.8 1.1 pad.4
  1.9 4.6 %while.24 = (s32[]{:T(128)}, bf16[4,16,2048]{2,1,0:T(8,128)(2,1)S(1)}, s32[4,16,32]{2,0,1:T(4,128)S(1)}, bf16[4,32,2056]{2,1,0:T(8,128)(2,1)S(1)}, s32[]{:T(128)}) while((s32[]{:T(128)}, bf16[4,16,2048]{2,1,0:T(8,128)(2,1)S(1)}, s32[4,16,32]{2,0,1:T(4,128)S(1)}, bf16[4,32,2056]{2,1,0:T(8,128)(2,1)S(1)}, s32[]{:T(128)}) %tuple.64), condition=%wide.region_1.2_spmd.clone, body=%wide.region_0.1_spmd.clone.sunk | while | flops 16814080 | bytes 3486793 | solution.py:46
  2.7 0.3 fusion.95
  3.9 0.3 fusion.95
  5.0 0.3 fusion.95
  6.2 0.3 fusion.95
  6.8 17.2 %all_to_all.5 = bf16[16,4,16,128]{3,2,1,0:T(8,128)(2,1)S(1)} all-to-all(bf16[16,4,16,128]{3,2,1,0:T(8,128)(2,1)S(1)} %constant_dynamic-update-slice_fusion.16), channel_id=1, replica_groups=mesh['beam'=2,'gx'=16] {'gx'}, dimensions={0} | all-to-all | bytes 524288 | tf_op jit(solution)/shard_map/all_to_all | solution.py:48
  24.1 1.3 collective-permute-start
  25.7 1.9 %collective-permute-done = bf16[64,16,32]{2,0,1:T(8,128)(2,1)S(1)} collective-permute-done((bf16[64,16,32]{2,0,1:T(8,128)(2,1)S(1)}, bf16[64,16,32]{2,0,1:T(8,128)(2,1)S(1)}, u32[]{:S(2)}, u32[]{:S(2)}) %collective-permute-start) | collective-permute-done | bytes 65568 | tf_op jit(solution)/shard_map/ppermute | solution.py:15
  27.7 70.5 %while.25 = (s32[]{:T(128)}, f32[16,96,128]{2,1,0:T(8,128)S(1)}, f32[16,16,96]{2,1,0:T(8,128)S(1)}, s32[16,96,64]{1,0,2:T(8,128)S(1)}, s32[16]{0:T(128)S(1)}, /*...) while((s32[]{:T(128)}, f32[16,96,128]{2,1,0:T(8,128)S(1)}, ...), condition=%wide.region_3.4_spmd.clone, body=%wide.region_2.3_spmd.clone.sunk | while | flops 28409860 | bytes 2107547 | solution.py:77
  27.7 0.6 dynamic_slice.38
  31.6 0.3 fusion.100
  31.9 0.2 fusion.101
  32.1 0.6 dynamic_slice.38
  36.0 0.3 fusion.100
  36.3 0.2 fusion.101
  36.5 0.6 dynamic_slice.38
  40.1 0.2 bitcast_compare_fusion.2
  40.4 0.3 fusion.100
  40.7 0.2 fusion.101
  40.9 0.6 dynamic_slice.38
  44.8 0.3 fusion.100
  45.1 0.2 fusion.101
  45.3 0.6 dynamic_slice.38
  49.2 0.3 fusion.100
  49.5 0.2 fusion.101
  49.7 0.6 dynamic_slice.38
  53.6 0.3 fusion.100
  53.9 0.2 fusion.101
  54.1 0.6 dynamic_slice.38
  58.0 0.3 fusion.100
  58.3 0.2 fusion.101
  58.5 0.6 dynamic_slice.38
  62.4 0.3 fusion.100
  62.7 0.2 fusion.101
  62.9 0.6 dynamic_slice.38
  66.8 0.3 fusion.100
  67.1 0.2 fusion.101
  67.3 0.6 dynamic_slice.38
  71.2 0.3 fusion.100
  71.5 0.2 fusion.101
  71.7 0.6 dynamic_slice.38
  75.6 0.3 fusion.100
  75.9 0.2 fusion.101
  76.2 0.6 dynamic_slice.38
  80.0 0.3 fusion.100
  80.3 0.2 fusion.101
  80.6 0.6 dynamic_slice.38
  84.4 0.3 fusion.100
  84.7 0.2 fusion.101
  85.0 0.6 dynamic_slice.38
  88.8 0.3 fusion.100
  89.1 0.2 fusion.101
  89.4 0.6 dynamic_slice.38
  93.2 0.3 fusion.100
  93.6 0.2 fusion.101
  93.8 0.6 dynamic_slice.38
  97.6 0.3 fusion.100
  98.0 0.2 fusion.101
  98.2 0.6 fusion.66
  99.0 0.3 copy.13
  99.2 61.7 %all-reduce.1 = (f32[1536]{0:T(1024)S(1)}, f32[1536]{0:T(1024)S(1)}) all-reduce(f32[1536]{0:T(1024)S(1)} %reduce_sum.25, f32[1536]{0:T(1024)S(1)} %reduce_sum.23), channel_id=1, replica_groups=mesh['beam'=2,'gx'=16] {'gx'}, use_global_device_ids=true, to_apply=%region_7.8 | all-reduce | flops 3072 | bytes 24576 | tf_op jit(solution)/shard_map/psum | solution.py:88
  160.9 11.9 %fusion.25 = f32[1536,128]{1,0:T(8,128)} fusion(f32[1536,128]{1,0:T(8,128)S(1)} %bitcast.254, f32[1536,16]{1,0:T(8,128)S(1)} %bitcast.253, f32[1536]{0:T(1024)S(1)} %get-tuple-element.136, f32[1536]{0:T(1024)S(1)} %get-tuple-element.135, pred[1536]{0:T(1024)(128)(4,1)S(1)} %get-tuple-element.152, pred[1536]{0:T(1024)(128)(4,1)S(1)} %get-tuple-element.138, ...), kind=kLoop, calls=%fused_computation.100 | loop fusion | flops 9437184 | bytes 1708032 | tf_op jit(solution)/shard_map/div | solution.py:94
  (406 shorter events, 28.4 us)
Async XLA Ops:
  6.5 18.9 %copy-start.1 = (s32[1536]{0:T(1024)S(1)}, s32[1536]{0:T(1024)}, u32[]{:S(2)}) copy-start(s32[1536]{0:T(1024)} %param.11) | copy-start | bytes 18436
  6.5 19.0 %copy-start = (s32[1536,64]{0,1:T(8,128)S(1)}, s32[1536,64]{0,1:T(8,128)}, u32[]{:S(2)}) copy-start(s32[1536,64]{0,1:T(8,128)} %param.10) | copy-start | bytes 1179652
  24.1 3.4 %collective-permute-start = (bf16[64,16,32]{2,0,1:T(8,128)(2,1)S(1)}, bf16[64,16,32]{2,0,1:T(8,128)(2,1)S(1)}, u32[]{:S(2)}, u32[]{:S(2)}) collective-permute-start(bf16[64,16,32]{2,0,1:T(8,128)(2,1)S(1)} %bitcast.256), channel_id=1, source_target_pairs={{1,0},{2,1},{3,2},{4,3},{5,4},{6,5},{7,6},{8,7},{9,8},{10,9},{11,1... | collective-permute-start | bytes 196616 | tf_op jit(solution)/shard_map/ppermute | solution.py:15
